TPU v7x, 32 devices: a whole 2x2x4 slice. The times are simulated.
32 devices in a mesh: grp: 2 (over y), seq: 4 (over z), head: 2 (over x), batch: 2 (over core).
Axes of the slice: x: 2, y: 2, z: 4, core: 2. Of those that a mesh axis runs over, the one named last changes fastest.
Arguments:
- queries: bfloat16 [64, 64, 128], P(('grp', 'batch'), 'head'), parts along dimension 0, may hold values from -8 to 8
- key_cache: bfloat16 [64, 8, 1024, 128], P(('grp', 'batch'), 'head', 'seq'), parts along dimension 0, may hold values from -5 to 5
- value_cache: bfloat16 [64, 8, 1024, 128], P(('grp', 'batch'), 'head', 'seq'), parts along dimension 0, may hold values from -5 to 5
- gate_logits: float32 [2, 64, 64], P(None, ('grp', 'batch'), 'head'), parts along dimension 1, may hold values from -6 to 6
- lengths: int32 [64], P(('grp', 'batch')), parts along dimension 0, may hold values from 256 to 1024, as said below
- chosen: int32 [64, 8, 2], P(('grp', 'batch'), 'head'), parts along dimension 0, may hold values from 0 to 7, as said below
- counts: int32 [64, 8], P(('grp', 'batch'), 'head'), parts along dimension 0, may hold values from 1 to 2, as said below
Outputs:
- output: bfloat16 [64, 64, 128], P(('grp', 'batch'), 'head'), parts along dimension 0
There are 2 independent parts, one for each index of `grp`. A program takes and returns all parts, laid end to end along the dimension named above; each array names one. Nothing has to cross between parts.
Inputs may be any that keep to these rules, and one draw needn't show every extreme that they name: `lengths`: every draw has a sequence of the full length 1024. `chosen`: for each sequence and key-value head the first counts entries are distinct blocks that start below the sequence's length, and the first entry is block 0; the entries after them are ignored. `counts`: every draw has a sequence with 2 valid entries for every key-value head.
All inputs are finite; a program needn't handle non-finite values.
Results may differ from a plain program's by a relative error of at most 0.02.
Values may be sent and summed in bfloat16 or wider, within the bound.
A program may use at most 64 MiB of HBM per device.

v0:
```python
import math
import jax
import jax.numpy as jnp
from jax import lax
from jax.sharding import PartitionSpec as P

BLOCK = 128


def combined_all(array, axis, join):
    gathered = jax.tree.map(
        lambda a, kind: lax.all_gather(a.astype(kind), axis),
        array,
        (jnp.bfloat16, jnp.bfloat16, jnp.bfloat16),
    )

    def take(source):
        return jax.tree.map(
            lambda a, own: lax.dynamic_index_in_dim(a, source, 0, False).astype(own.dtype),
            gathered,
            array,
        )

    return lax.fori_loop(
        1, lax.axis_size(axis), lambda source, state: join(state, take(source)), take(0)
    )


def softmax_terms(query_rows, key_rows, value_rows, live_mask, score_scale):
    scores = (
        jnp.einsum("pgd,pnd->pgn", query_rows, key_rows, preferred_element_type=jnp.float32)
        * score_scale
    )
    scores = jnp.where(live_mask[:, None, :], scores, -1e30)
    row_max = jnp.max(scores, axis=2)
    weights = jnp.where(live_mask[:, None, :], jnp.exp(scores - row_max[:, :, None]), 0.0)
    weight_sum = jnp.sum(weights, axis=2)
    summed = jnp.einsum(
        "pgn,pnd->pgd", weights.astype(jnp.bfloat16), value_rows, preferred_element_type=jnp.float32
    )
    return (row_max, weight_sum, summed)


def combine(first, second):
    merged = []
    for index in range(0, len(first), 3):
        row_max = jnp.maximum(first[index], second[index])
        factor_first = jnp.exp(first[index] - row_max)
        factor_second = jnp.exp(second[index] - row_max)
        merged.append(row_max)
        merged.append(first[index + 1] * factor_first + second[index + 1] * factor_second)
        merged.append(
            first[index + 2] * factor_first[:, :, None]
            + second[index + 2] * factor_second[:, :, None]
        )
    return tuple(merged)


def finish(weight_sum, summed):
    return summed / weight_sum[:, :, None]


def pool_blocks(key_rows, value_rows, pair_lengths, first_block):
    pair_count, tokens, head_width = key_rows.shape
    block_count = tokens // BLOCK
    position = first_block * BLOCK + jnp.arange(tokens, dtype=jnp.int32)
    live_mask = position[None, :] < pair_lengths[:, None]
    token_ones = live_mask.astype(jnp.bfloat16).reshape(pair_count, block_count, BLOCK)
    starts = (first_block + jnp.arange(block_count, dtype=jnp.int32)) * BLOCK
    filled = jnp.clip(pair_lengths[:, None] - starts[None, :], 0, BLOCK)
    root_fill = jnp.sqrt(jnp.maximum(filled, 1).astype(jnp.float32))[:, :, None]
    key_sums = jnp.einsum(
        "pjt,pjtd->pjd",
        token_ones,
        key_rows.reshape(pair_count, block_count, BLOCK, head_width),
        preferred_element_type=jnp.float32,
    )
    value_sums = jnp.einsum(
        "pjt,pjtd->pjd",
        token_ones,
        value_rows.reshape(pair_count, block_count, BLOCK, head_width),
        preferred_element_type=jnp.float32,
    )
    pooled_keys = (key_sums / root_fill).astype(jnp.bfloat16)
    pooled_values = (value_sums / root_fill).astype(jnp.bfloat16)
    return (live_mask, filled > 0, pooled_keys, pooled_values)


def picked_tokens(live_mask, chosen_rows, count_rows, first_block):
    pair_count, tokens = live_mask.shape
    block_count = tokens // BLOCK
    block_ids = first_block + jnp.arange(block_count, dtype=jnp.int32)
    slot_live = jnp.arange(chosen_rows.shape[1], dtype=jnp.int32)[None, :] < count_rows[:, None]
    picked = jnp.any(
        (chosen_rows[:, :, None] == block_ids[None, None, :]) & slot_live[:, :, None], axis=1
    )
    spread = jnp.broadcast_to(picked[:, :, None], (pair_count, block_count, BLOCK)).reshape(
        pair_count, tokens
    )
    return live_mask & spread


def blend_gates(compressed, selected, gate_pairs):
    mixed = gate_pairs[0][:, :, None] * compressed + gate_pairs[1][:, :, None] * selected
    return mixed.astype(jnp.bfloat16)


def on_device(queries, key_cache, value_cache, gate_logits, lengths, chosen, counts):
    batch_rows, head_count, context, head_width = key_cache.shape
    pair_count = batch_rows * head_count
    group_size = queries.shape[1] // head_count
    score_scale = 1.0 / math.sqrt(head_width)
    query_rows = queries.reshape(pair_count, group_size, head_width)
    pair_keys = key_cache.reshape(pair_count, context, head_width)
    pair_values = value_cache.reshape(pair_count, context, head_width)
    pair_lengths = jnp.broadcast_to(lengths[:, None], (batch_rows, head_count)).reshape(pair_count)
    pair_chosen = chosen.reshape(pair_count, chosen.shape[2])
    pair_counts = counts.reshape(pair_count)
    gate_pairs = jax.nn.sigmoid(gate_logits.reshape(2, pair_count, group_size))
    local_blocks = context // BLOCK
    first_block = lax.axis_index("seq") * local_blocks
    live_mask, block_live, pooled_keys, pooled_values = pool_blocks(
        pair_keys, pair_values, pair_lengths, first_block
    )
    token_mask = picked_tokens(live_mask, pair_chosen, pair_counts, first_block)
    all_keys, all_values = (
        lax.all_gather(pooled_keys, "seq", axis=1, tiled=True),
        lax.all_gather(pooled_values, "seq", axis=1, tiled=True),
    )
    all_starts = jnp.arange(all_keys.shape[1], dtype=jnp.int32) * BLOCK
    all_live = all_starts[None, :] < pair_lengths[:, None]
    s_max, s_sum, s_val = softmax_terms(query_rows, pair_keys, pair_values, token_mask, score_scale)
    merged = combined_all((s_max, s_sum, s_val), "seq", combine)
    c_max, c_sum, c_val = softmax_terms(query_rows, all_keys, all_values, all_live, score_scale)
    output = blend_gates(finish(c_sum, c_val), finish(merged[1], merged[2]), gate_pairs)
    return output.reshape(batch_rows, head_count * group_size, head_width)


def solution(mesh):
    return jax.shard_map(
        on_device,
        mesh=mesh,
        in_specs=(
            P(("grp", "batch"), "head", None),
            P(("grp", "batch"), "head", "seq", None),
            P(("grp", "batch"), "head", "seq", None),
            P(None, ("grp", "batch"), "head"),
            P(("grp", "batch")),
            P(("grp", "batch"), "head", None),
            P(("grp", "batch"), "head"),
        ),
        out_specs=P(("grp", "batch"), "head", None),
        check_vma=False,
    )
```

profile of v0, /device:TPU:0, one launch (start us, length us, event | category | flops | bytes accessed | tf_op | source)
XLA Modules:
  0.0 87.3 jit_solution(7308756827463599597)
XLA Ops:
  0.0 0.9 %copy-done = bf16[16,32,128]{2,1,0:T(8,128)(2,1)S(1)} copy-done((bf16[16,32,128]{2,1,0:T(8,128)(2,1)S(1)}, bf16[16,32,128]{2,1,0:T(8,128)(2,1)}, u32[]{:S(2)}) %copy-start) | copy-done | bytes 131096
  0.9 0.7 broadcast_in_dim.71
  1.7 0.1 compare_bitcast_fusion
  1.9 3.4 %fusion.17 = f32[64,2,1,128]{3,2,1,0:T(1,128)S(1)} fusion(bf16[64,2,128,128]{3,2,1,0:T(8,128)(2,1)} %bitcast.70, pred[64,2,128,1]{2,1,0,3:T(4,128)(4,1)S(1)} %compare_bitcast_fusion), kind=kOutput, calls=%fused_computation.25 | convolution fusion | flops 4194304 | bytes 4276224 | tf_op jit(solution)/shard_map/pjt,pjtd->pjd/dot_general | solution.py:78
  5.4 3.4 %fusion.19 = f32[64,2,1,128]{3,2,1,0:T(1,128)S(1)} fusion(bf16[64,2,128,128]{3,2,1,0:T(8,128)(2,1)} %bitcast.68, pred[64,2,128,1]{2,1,0,3:T(4,128)(4,1)S(1)} %compare_bitcast_fusion), kind=kOutput, calls=%fused_computation.27 | convolution fusion | flops 4194304 | bytes 4276224 | tf_op jit(solution)/shard_map/pjt,pjtd->pjd/dot_general | solution.py:72
  8.8 0.1 fusion.24
  8.9 15.1 %all_gather.20 = bf16[64,8,128]{2,0,1:T(8,128)(2,1)S(1)} all-gather(bf16[64,2,128]{2,0,1:T(8,128)(2,1)S(1)} %get-tuple-element.207), channel_id=1, replica_groups=mesh['grp'=2,'seq'=4,'head'=2,'batch'=2] {'seq'}, dimensions={1}, use_global_device_ids=true | all-gather | bytes 163840 | tf_op jit(solution)/shard_map/all_gather | solution.py:127
  24.0 0.2 fusion.22
  24.2 0.1 copy.61
  24.4 0.1 copy.62
  25.1 0.1 copy.67
  25.2 0.1 broadcast_in_dim.76
  25.4 3.5 %fusion.38 = (f32[64,8]{1,0:T(8,128)S(1)}, f32[64,8,256]{2,1,0:T(8,128)S(1)}) fusion(bf16[64,8,128]{2,1,0:T(8,128)(2,1)S(1)} %bitcast.67, bf16[64,256,128]{2,1,0:T(8,128)(2,1)} %bitcast.69, pred[64,256]{1,0:T(8,128)(4,1)S(1)} %bitcast_and_fusion), kind=kOutput, calls=%fused_computation.66 | convolution fusion | flops 33947136 | bytes 4868096 | tf_op jit(solution)/shard_map/pgd,pnd->pgn/dot_general | solution.py:31
  29.0 11.9 %all-gather.3 = bf16[4,64,8]{1,2,0:T(8,128)(2,1)S(1)} all-gather(bf16[1,64,8]{1,2,0:T(8,128)(2,1)S(1)} %copy.68), channel_id=2, replica_groups=mesh['grp'=2,'seq'=4,'head'=2,'batch'=2] {'seq'}, dimensions={0}, use_global_device_ids=true | all-gather | bytes 5120 | tf_op jit(solution)/shard_map/all_gather | solution.py:12
  40.9 0.3 fusion.12
  41.2 11.9 %all-gather.4 = bf16[4,64,8]{1,2,0:T(8,128)(2,1)S(1)} all-gather(bf16[1,64,8]{1,2,0:T(8,128)(2,1)S(1)} %copy.69), channel_id=3, replica_groups=mesh['grp'=2,'seq'=4,'head'=2,'batch'=2] {'seq'}, dimensions={0}, use_global_device_ids=true | all-gather | bytes 5120 | tf_op jit(solution)/shard_map/all_gather | solution.py:12
  53.2 2.9 %convolution_convert_fusion = bf16[64,8,128]{2,1,0:T(8,128)(2,1)S(1)} fusion(bf16[64,256,128]{2,1,0:T(8,128)(2,1)} %bitcast.71, f32[64,8,256]{2,1,0:T(8,128)S(1)} %get-tuple-element.210, f32[64,8]{1,0:T(8,128)S(1)} %get-tuple-element.209, pred[64,256]{1,0:T(8,128)(4,1)S(1)} %bitcast_and_fusion), kind=kOutput, calls=%fused_computation.15 | convolution fusion | flops 34013184 | bytes 4868096 | tf_op jit(solution)/shard_map/pgn,pnd->pgd/dot_general | solution.py:38
  56.1 15.0 %all-gather.2 = bf16[256,8,128]{2,1,0:T(8,128)(2,1)S(1)} all-gather(bf16[64,8,128]{2,1,0:T(8,128)(2,1)S(1)} %convolution_convert_fusion), channel_id=4, replica_groups=mesh['grp'=2,'seq'=4,'head'=2,'batch'=2] {'seq'}, dimensions={0}, use_global_device_ids=true | all-gather | bytes 655360 | tf_op jit(solution)/shard_map/all_gather | solution.py:12
  71.1 1.5 %while.19 = (s32[]{:T(128)}, f32[64,8]{0,1:T(8,128)S(1)}, f32[64,8]{0,1:T(8,128)S(1)}, f32[64,8,128]{2,1,0:T(8,128)S(1)}, bf16[4,64,8]{1,2,0:T(8,128)(2,1)S(1)},...) while((s32[]{:T(128)}, f32[64,8]{0,1:T(8,128)S(1)}, ...), condition=%wide.region_6.7_spmd, body=%wide.region_5.6_spmd.sunk | while | flops 266245 | bytes 682135 | solution.py:24
  71.3 0.3 fusion.49
  71.8 0.3 fusion.49
  72.3 0.3 fusion.49
  72.6 13.3 %all_gather.21 = bf16[64,8,128]{2,0,1:T(8,128)(2,1)S(1)} all-gather(bf16[64,2,128]{2,0,1:T(8,128)(2,1)S(1)} %get-tuple-element.206), channel_id=1, replica_groups=mesh['grp'=2,'seq'=4,'head'=2,'batch'=2] {'seq'}, dimensions={1}, use_global_device_ids=true | all-gather | bytes 163840 | tf_op jit(solution)/shard_map/all_gather | solution.py:128
  86.3 1.0 %fusion.7 = bf16[64,8,128]{2,1,0:T(8,128)(2,1)} fusion(bf16[64,8,8]{2,1,0:T(8,128)(2,1)S(1)} %copy.62, f32[64,8,128]{2,1,0:T(8,128)S(1)} %get-tuple-element.182, bf16[64,8,128]{2,0,1:T(8,128)(2,1)S(1)} %all_gather.21, f32[64,8]{1,0:T(8,128)S(1)} %copy.70, f32[64,8]{1,0:T(8,128)S(1)} %mul.134, f32[64,8]{1,0:T(8,128)S(1)} %copy.64, f32[64,8]{1,0:T(8,128)S(1)} %mul.125), kind=kOutput, calls=%fused_computation.14 | convolution fusion | flops 1441792 | bytes 540672 | tf_op jit(solution)/shard_map/pgn,pnd->pgd/dot_general | solution.py:38
  (43 shorter events, 1.9 us)
Async XLA Ops:
  0.0 0.9 %copy-start = (bf16[16,32,128]{2,1,0:T(8,128)(2,1)S(1)}, bf16[16,32,128]{2,1,0:T(8,128)(2,1)}, u32[]{:S(2)}) copy-start(bf16[16,32,128]{2,1,0:T(8,128)(2,1)} %param.9) | copy-start | bytes 393220
  1.9 22.7 %copy-start.3 = (s32[16,4]{0,1:T(4,128)S(1)}, s32[16,4]{0,1:T(4,128)}, u32[]{:S(2)}) copy-start(s32[16,4]{0,1:T(4,128)} %param.15) | copy-start | bytes 772
  1.9 22.9 %copy-start.2 = (s32[16,4,2]{0,2,1:T(2,128)S(1)}, s32[16,4,2]{0,2,1:T(2,128)}, u32[]{:S(2)}) copy-start(s32[16,4,2]{0,2,1:T(2,128)} %param.14) | copy-start | bytes 1540
  53.2 32.9 %copy-start.1 = (f32[2,16,32]{2,1,0:T(8,128)S(1)}, f32[2,16,32]{2,1,0:T(8,128)}, u32[]{:S(2)}) copy-start(f32[2,16,32]{2,1,0:T(8,128)} %param.12) | copy-start | bytes 12292
where the time goes:
time: 87.6 us; the launch traced here: 87.3 us
  blocking collectives  67.3 us (77%)
  matrix products  14.3 us (16%)
  local copies, waits for them, and re-layouts  3.58 us (4%)
  other arithmetic  1.83 us (2%)
    all_gather x3, blocking collectives, combined_all(): lax.all_gather(a.astype(kind), axis)  38.9 us
    all_gather x1, blocking collectives, on_device(): lax.all_gather(pooled_keys, 'seq', axis=1, tiled=True)  15.1 us
    all_gather x1, blocking collectives, on_device(): lax.all_gather(pooled_values, 'seq', axis=1, tiled=True)  13.3 us
    dot_general x2, matrix products, softmax_terms(): jnp.einsum('pgn,pnd->pgd', weights.astype(jnp.bfloat16), value_rows, pref...  3.93 us
    dot_general x2, matrix products, softmax_terms(): jnp.einsum('pgd,pnd->pgn', query_rows, key_rows, preferred_element_type=j...  3.65 us
    dot_general x1, matrix products, pool_blocks(): jnp.einsum('pjt,pjtd->pjd', token_ones, key_rows.reshape(pair_count, bloc...  3.39 us
    dot_general x1, matrix products, pool_blocks(): jnp.einsum('pjt,pjtd->pjd', token_ones, value_rows.reshape(pair_count, bl...  3.38 us

commit v1 on v0

--- a/solution.py
+++ b/solution.py
@@ -125,7 +125,7 @@
     token_mask = picked_tokens(live_mask, pair_chosen, pair_counts, first_block)
     all_keys, all_values = (
         lax.all_gather(pooled_keys, "seq", axis=1, tiled=True),
-        lax.all_gather(pooled_values, "seq", axis=1, tiled=True),
+        jnp.concatenate(lax.all_gather(pooled_values, "seq"), axis=1),
     )
     all_starts = jnp.arange(all_keys.shape[1], dtype=jnp.int32) * BLOCK
     all_live = all_starts[None, :] < pair_lengths[:, None]

time: 87.6 us -> 85 us (0.970)
  matrix products: 14.3 us -> 10.3 us
  blocking collectives: 67.3 us -> 68.3 us
    all_gather x3, blocking collectives: 38.9 us -> 41.6 us  [combined_all(): lax.all_gather(a.astype(kind), axis)]
    dot_general x1, matrix products: 3.39 us -> 1.2 us  [pool_blocks(): jnp.einsum('pjt,pjtd->pjd', token_ones, key_rows.reshape(pair_count, bloc...]
    dot_general x2, matrix products: 3.93 us -> 1.74 us  [softmax_terms(): jnp.einsum('pgn,pnd->pgd', weights.astype(jnp.bfloat16), value_rows, pref...]
    all_gather x1, blocking collectives: 15.1 us -> 13.3 us  [on_device(): lax.all_gather(pooled_keys, 'seq', axis=1, tiled=True)]
where the time goes in v1:
time: 85 us; the launch traced here: 84.8 us
  blocking collectives  68.3 us (80%)
  matrix products  10.3 us (12%)
  local copies, waits for them, and re-layouts  4.19 us (5%)
  other arithmetic  1.82 us (2%)
    all_gather x3, blocking collectives, combined_all(): lax.all_gather(a.astype(kind), axis)  41.6 us
    all_gather x1, blocking collectives, on_device(): lax.all_gather(pooled_keys, 'seq', axis=1, tiled=True)  13.3 us
    all_gather x1, blocking collectives, on_device(): lax.all_gather(pooled_values, 'seq')  13.3 us
    dot_general x2, matrix products, softmax_terms(): jnp.einsum('pgd,pnd->pgn', query_rows, key_rows, preferred_element_type=j...  3.8 us
    dot_general x1, matrix products, pool_blocks(): jnp.einsum('pjt,pjtd->pjd', token_ones, value_rows.reshape(pair_count, bl...  3.53 us
    dot_general x2, matrix products, softmax_terms(): jnp.einsum('pgn,pnd->pgd', weights.astype(jnp.bfloat16), value_rows, pref...  1.74 us

profile of v1, /device:TPU:0, one launch (start us, length us, event | category | flops | bytes accessed | tf_op | source)
XLA Modules:
  0.0 84.8 jit_solution(8849865567421725002)
XLA Ops:
  0.0 0.8 broadcast_in_dim.71
  0.9 0.8 copy.71
  1.7 0.8 copy.72
  2.7 0.1 copy.73
  2.8 0.1 broadcast_in_dim.76
  3.1 3.6 %fusion.37 = (f32[64,8]{1,0:T(8,128)S(1)}, f32[64,8,256]{2,1,0:T(8,128)S(1)}) fusion(bf16[64,8,128]{2,1,0:T(8,128)(2,1)S(1)} %bitcast.72, bf16[64,256,128]{2,1,0:T(8,128)(2,1)} %bitcast.75, pred[64,256]{1,0:T(8,128)(4,1)S(1)} %bitcast_and_fusion), kind=kOutput, calls=%fused_computation.65 | convolution fusion | flops 33947136 | bytes 4868096 | tf_op jit(solution)/shard_map/pgd,pnd->pgn/dot_general | solution.py:31
  6.7 0.7 convolution_convert_fusion
  7.4 17.4 %all-gather.3 = bf16[256,8,128]{2,1,0:T(8,128)(2,1)S(1)} all-gather(bf16[64,8,128]{2,1,0:T(8,128)(2,1)S(1)} %convolution_convert_fusion), channel_id=5, replica_groups=mesh['grp'=2,'seq'=4,'head'=2,'batch'=2] {'seq'}, dimensions={0}, use_global_device_ids=true | all-gather | bytes 655360 | tf_op jit(solution)/shard_map/all_gather | solution.py:12
  24.8 0.3 fusion.12
  25.1 12.3 %all-gather.5 = bf16[4,64,8]{1,2,0:T(8,128)(2,1)S(1)} all-gather(bf16[1,64,8]{1,2,0:T(8,128)(2,1)S(1)} %copy.75), channel_id=4, replica_groups=mesh['grp'=2,'seq'=4,'head'=2,'batch'=2] {'seq'}, dimensions={0}, use_global_device_ids=true | all-gather | bytes 5120 | tf_op jit(solution)/shard_map/all_gather | solution.py:12
  37.5 11.9 %all-gather.4 = bf16[4,64,8]{1,2,0:T(8,128)(2,1)S(1)} all-gather(bf16[1,64,8]{1,2,0:T(8,128)(2,1)S(1)} %copy.74), channel_id=3, replica_groups=mesh['grp'=2,'seq'=4,'head'=2,'batch'=2] {'seq'}, dimensions={0}, use_global_device_ids=true | all-gather | bytes 5120 | tf_op jit(solution)/shard_map/all_gather | solution.py:12
  49.4 1.5 %while.19 = (s32[]{:T(128)}, f32[64,8]{0,1:T(8,128)S(1)}, f32[64,8]{0,1:T(8,128)S(1)}, f32[64,8,128]{2,1,0:T(8,128)S(1)}, bf16[4,64,8]{1,2,0:T(8,128)(2,1)S(1)},...) while((s32[]{:T(128)}, f32[64,8]{0,1:T(8,128)S(1)}, ...), condition=%wide.region_6.7_spmd, body=%wide.region_5.6_spmd.sunk | while | flops 266245 | bytes 682135 | solution.py:24
  49.6 0.3 fusion.49
  50.1 0.3 fusion.49
  50.6 0.3 fusion.49
  51.0 0.1 compare_bitcast_fusion
  51.1 3.5 %fusion.17 = f32[64,2,1,128]{3,2,1,0:T(1,128)S(1)} fusion(bf16[64,2,128,128]{3,2,1,0:T(8,128)(2,1)} %bitcast.73, pred[64,2,128,1]{2,1,0,3:T(4,128)(4,1)S(1)} %compare_bitcast_fusion), kind=kOutput, calls=%fused_computation.25 | convolution fusion | flops 4194304 | bytes 4276224 | tf_op jit(solution)/shard_map/pjt,pjtd->pjd/dot_general | solution.py:78
  54.6 1.2 %fusion.19 = f32[64,2,1,128]{3,2,1,0:T(1,128)S(1)} fusion(bf16[64,2,128,128]{3,2,1,0:T(8,128)(2,1)S(1)} %bitcast.76, pred[64,2,128,1]{2,1,0,3:T(4,128)(4,1)S(1)} %compare_bitcast_fusion), kind=kOutput, calls=%fused_computation.27 | convolution fusion | flops 4194304 | bytes 4276224 | tf_op jit(solution)/shard_map/pjt,pjtd->pjd/dot_general | solution.py:72
  56.0 13.3 %all_gather.23 = bf16[64,8,128]{2,0,1:T(8,128)(2,1)S(1)} all-gather(bf16[64,2,128]{2,0,1:T(8,128)(2,1)S(1)} %get-tuple-element.207), channel_id=1, replica_groups=mesh['grp'=2,'seq'=4,'head'=2,'batch'=2] {'seq'}, dimensions={1}, use_global_device_ids=true | all-gather | bytes 163840 | tf_op jit(solution)/shard_map/all_gather | solution.py:127
  69.4 0.2 fusion.21
  69.6 0.1 copy.66
  69.9 0.1 copy.69
  70.1 13.3 %all-gather = bf16[256,2,128]{2,1,0:T(2,128)(2,1)S(1)} all-gather(bf16[64,2,128]{2,1,0:T(2,128)(2,1)S(1)} %copy.67), channel_id=2, replica_groups=mesh['grp'=2,'seq'=4,'head'=2,'batch'=2] {'seq'}, dimensions={0}, use_global_device_ids=true | all-gather | bytes 163840 | tf_op jit(solution)/shard_map/all_gather | solution.py:128
  83.8 1.0 %fusion.7 = bf16[64,8,128]{2,1,0:T(8,128)(2,1)} fusion(bf16[64,8,8]{2,1,0:T(8,128)(2,1)S(1)} %copy.69, bf16[64,8,128]{2,1,0:T(8,128)(2,1)S(1)} %bitcast.80, f32[64,8,128]{2,1,0:T(8,128)S(1)} %get-tuple-element.182, f32[64,8]{1,0:T(8,128)S(1)} %copy.76, f32[64,8]{1,0:T(8,128)S(1)} %mul.134, f32[64,8]{1,0:T(8,128)S(1)} %copy.70, f32[64,8]{1,0:T(8,128)S(1)} %mul.125), kind=kOutput, calls=%fused_computation.14 | convolution fusion | flops 1441792 | bytes 540672 | tf_op jit(solution)/shard_map/pgn,pnd->pgd/dot_general | solution.py:38
  (45 shorter events, 2.0 us)
Async XLA Ops:
  0.0 3.1 %copy-start = (bf16[16,32,128]{2,1,0:T(8,128)(2,1)S(1)}, bf16[16,32,128]{2,1,0:T(8,128)(2,1)}, u32[]{:S(2)}) copy-start(bf16[16,32,128]{2,1,0:T(8,128)(2,1)} %param.9) | copy-start | bytes 393220
  2.9 3.7 %copy-start.1 = (bf16[16,4,256,128]{3,2,1,0:T(8,128)(2,1)S(1)}, bf16[16,4,256,128]{3,2,1,0:T(8,128)(2,1)}, u32[]{:S(2)}) copy-start(bf16[16,4,256,128]{3,2,1,0:T(8,128)(2,1)} %param.11) | copy-start | bytes 12582916
  51.0 3.7 %copy-start.2 = (bf16[16,4,256,128]{3,2,1,0:T(8,128)(2,1)S(1)}, bf16[16,4,256,128]{3,2,1,0:T(8,128)(2,1)}, u32[]{:S(2)}) copy-start(bf16[16,4,256,128]{3,2,1,0:T(8,128)(2,1)} %param.10) | copy-start | bytes 12582916
  54.6 28.9 %copy-start.3 = (f32[2,16,32]{2,1,0:T(8,128)S(1)}, f32[2,16,32]{2,1,0:T(8,128)}, u32[]{:S(2)}) copy-start(f32[2,16,32]{2,1,0:T(8,128)} %param.12) | copy-start | bytes 12292
